TPU v7x, 32 devices: a whole 2x2x4 slice. The times are simulated.
32 devices in a mesh: expert: 4 (over y, core), shard: 8 (over z, x).
Axes of the slice: x: 2, y: 2, z: 4, core: 2. Of those that a mesh axis runs over, the one named last changes fastest.
Arguments:
- train_down: float32 [16, 6400, 4096], P('expert', None, 'shard'), may hold values from -0.109375 to 0.109375
- other_down: bfloat16 [16, 6400, 4096], P('expert', None, 'shard'), may hold values from -0.0390625 to 0.0390625
- router_weight: float32 [4096, 16], P('shard', 'expert'), may hold values from -0.09375 to 0.09375
- router_gain: float32 [4096], P('shard'), may hold values from 0.25 to 1.75
Outputs:
- ready_down: bfloat16 [16, 6400, 4096], P('expert', 'shard')
- scale_down: float32 [16, 6400], P('expert', 'shard')
- serve_router: bfloat16 [4096, 16], replicated
All inputs are finite; a program needn't handle non-finite values.
Results may differ from a plain program's by a relative error of at most 0.001.
Values may be sent and summed in bfloat16 or wider, within the bound.
A program may use at most 256 MiB of HBM per device.

v0:
```python
import functools

import jax
import jax.numpy as jnp
from jax import lax
from jax.experimental import pallas as pl
from jax.experimental.pallas import tpu as pltpu
from jax.sharding import PartitionSpec as P


def partner(me, k, n):
    other, bit = me, 1
    while bit < n:
        if k & bit:
            other = other + bit * (1 - 2 * (lax.div(me, bit) % 2))
        bit *= 2
    return other


def exchange_kernel(n, narrow_ref, out_ref, send_sem, recv_sem, own_sem):
    me = lax.axis_index("shard")
    rows, width = out_ref.shape[1], narrow_ref.shape[2]
    partners = [partner(me, k, n) for k in range(1, n)]

    barrier = pltpu.get_barrier_semaphore()
    for other in partners:
        pl.semaphore_signal(
            barrier, inc=1, device_id={"shard": other}, device_id_type=pl.DeviceIdType.MESH
        )
    pl.semaphore_wait(barrier, n - 1)

    columns = pl.ds(pl.multiple_of(me * width, 128), width)

    def rows_of(device):
        return pl.ds(pl.multiple_of(device * rows, 16), rows)

    copies = []
    for k, other in enumerate(partners):
        copy = pltpu.make_async_remote_copy(
            src_ref=narrow_ref.at[:, rows_of(other), :],
            dst_ref=out_ref.at[:, :, columns],
            send_sem=send_sem.at[k],
            recv_sem=recv_sem.at[k],
            device_id={"shard": other},
            device_id_type=pl.DeviceIdType.MESH,
        )
        copy.start()
        copies.append(copy)
    own = pltpu.make_async_copy(
        narrow_ref.at[:, rows_of(me), :], out_ref.at[:, :, columns], own_sem
    )
    own.start()
    own.wait()
    for copy in copies:
        copy.wait()


def exchange(narrow_down, n):
    experts, inner, width = narrow_down.shape
    return pl.pallas_call(
        functools.partial(exchange_kernel, n),
        out_shape=jax.ShapeDtypeStruct((experts, inner // n, width * n), narrow_down.dtype),
        in_specs=[pl.BlockSpec(memory_space=pl.ANY)],
        out_specs=pl.BlockSpec(memory_space=pl.ANY),
        scratch_shapes=[
            pltpu.SemaphoreType.DMA((n - 1,)),
            pltpu.SemaphoreType.DMA((n - 1,)),
            pltpu.SemaphoreType.DMA,
        ],
        compiler_params=pltpu.CompilerParams(collective_id=0, has_side_effects=True),
        name="exchange",
    )(narrow_down)


def per_device(n, train_down, other_down, router_weight, router_gain):
    latest_down = train_down + other_down.astype(jnp.float32)
    part_down = jnp.sum(latest_down * latest_down, axis=2)
    total_down = jnp.sum(lax.all_gather(part_down, "shard", axis=0), axis=0)
    scale_down = jnp.sqrt(total_down)
    narrow_down = (latest_down / jnp.expand_dims(scale_down, 2)).astype(jnp.bfloat16)
    ready_down = exchange(narrow_down, n)
    scale_down = lax.dynamic_slice_in_dim(
        scale_down, lax.axis_index("shard") * ready_down.shape[1], ready_down.shape[1], axis=1
    )
    part_router = (router_weight * router_gain[:, None]).astype(jnp.bfloat16)
    row_router = lax.all_gather(part_router, "shard", axis=0, tiled=True)
    serve_router = lax.all_gather(row_router, "expert", axis=1, tiled=True)
    return (ready_down, scale_down, serve_router)


def solution(mesh):
    in_specs = (
        P("expert", None, "shard"),
        P("expert", None, "shard"),
        P("shard", "expert"),
        P("shard"),
    )
    out_specs = (P("expert", "shard", None), P("expert", "shard"), P())
    return jax.shard_map(
        functools.partial(per_device, mesh.shape["shard"]),
        mesh=mesh,
        in_specs=in_specs,
        out_specs=out_specs,
        check_vma=False,
    )
```

profile of v0, /device:TPU:0, one launch (start us, length us, event | category | flops | bytes accessed | tf_op | source)
XLA Modules:
  0.0 707.8 jit_solution(1934832086001310032)
XLA Ops:
  0.6 24.2 %multiply_reduce_fusion = f32[4,6400]{1,0:T(4,128)S(1)} fusion(f32[4,6400,512]{2,1,0:T(8,128)} %param.4, bf16[4,6400,512]{2,1,0:T(8,128)(2,1)} %param.5), kind=kLoop, calls=%fused_computation.1 | loop fusion | flops 52403200 | bytes 78745600 | tf_op jit(solution)/shard_map/reduce_sum | solution.py:77
  24.9 33.9 %all-gather.1 = f32[8,4,6400]{2,1,0:T(4,128)S(1)} all-gather(f32[1,4,6400]{2,1,0:T(4,128)S(1)} %bitcast.5), channel_id=2, replica_groups=mesh['expert'=4,'shard'=8] {'shard'}, dimensions={0}, use_global_device_ids=true | all-gather | bytes 921600 | tf_op jit(solution)/shard_map/all_gather | solution.py:78
  58.8 0.1 reduce_sum.19
  58.9 0.1 sqrt.7
  59.0 0.7 constant_dynamic-slice_fusion
  59.7 34.3 %divide_convert_fusion.narrow_ref = bf16[4,6400,512]{2,1,0:T(8,128)(2,1)} fusion(f32[4,6400,512]{2,1,0:T(8,128)} %param.4, bf16[4,6400,512]{2,1,0:T(8,128)(2,1)} %param.5, f32[4,6400]{1,0:T(4,128)S(1)} %sqrt.7), kind=kLoop, calls=%fused_computation | loop fusion | flops 52428800 | bytes 104960000 | tf_op jit(solution)/shard_map/convert_element_type | solution.py:80
  93.9 0.0 copy-start
  93.9 0.0 copy-start.1
  93.9 428.1 %exchange.1 = bf16[4,800,4096]{2,1,0:T(8,128)(2,1)} custom-call(bf16[4,6400,512]{2,1,0:T(8,128)(2,1)} %divide_convert_fusion.narrow_ref), custom_call_target="tpu_custom_call" | custom-call | tf_op jit(solution)/shard_map/exchange/pallas_call | solution.py:60
  522.1 0.0 copy-done
  522.1 0.0 copy-done.1
  522.1 161.6 %all_gather.14 = bf16[4096,4]{0,1:T(4,128)(2,1)S(1)} all-gather(bf16[512,4]{0,1:T(4,128)(2,1)S(1)} %multiply_convert_fusion), channel_id=1, replica_groups=mesh['expert'=4,'shard'=8] {'shard'}, dimensions={0}, use_global_device_ids=true | all-gather | bytes 36864 | tf_op jit(solution)/shard_map/all_gather | solution.py:86
  683.7 5.4 all-gather.2
  689.1 0.7 reshape.14
  689.8 17.9 %copy.8 = bf16[4,800,4096]{2,1,0:T(8,128)(2,1)} copy(bf16[4,800,4096]{2,1,0:T(8,128)(2,1)} %exchange.1) | data formatting | bytes 52428800
  (1 shorter events, 0.0 us)
Async XLA Ops:
  93.9 428.1 %copy-start = (f32[512,4]{0,1:T(4,128)S(1)}, f32[512,4]{0,1:T(4,128)}, u32[]{:S(2)}) copy-start(f32[512,4]{0,1:T(4,128)} %param.6) | copy-start | bytes 24580
  93.9 428.2 %copy-start.1 = (f32[512]{0:T(512)S(1)}, f32[512]{0:T(512)}, u32[]{:S(2)}) copy-start(f32[512]{0:T(512)} %param.7) | copy-start | bytes 6148
where the time goes:
time: 708 us
  Pallas kernels  428 us (60%)
  blocking collectives  201 us (28%)
  other arithmetic  58.6 us (8%)
  local copies, waits for them, and re-layouts  19.4 us (3%)
    pallas_call x1, Pallas kernels, exchange(): pl.pallas_call(functools.partial(exchange_kernel, n), out_shape=jax.Shape...  428 us
    all_gather x1, blocking collectives, per_device(): row_router = lax.all_gather(part_router, 'shard', axis=0, tiled=True)  162 us
    convert_element_type x1, other arithmetic, per_device(): (latest_down / jnp.expand_dims(scale_down, 2)).astype(jnp.bfloat16)  34.3 us
    all_gather x1, blocking collectives, per_device(): total_down = jnp.sum(lax.all_gather(part_down, 'shard', axis=0), axis=0)  33.9 us
    reduce_sum x1, other arithmetic, per_device(): part_down = jnp.sum(latest_down * latest_down, axis=2)  24.2 us
    unnamed x6, local copies, waits for them, and re-layouts  18.6 us

commit v1 on v0

v1 whole, which is shorter than its diff:
```python
import functools

import jax
import jax.numpy as jnp
from jax import lax
from jax.experimental import pallas as pl
from jax.experimental.pallas import tpu as pltpu
from jax.sharding import PartitionSpec as P

LANES = 128
RING = 4
SLOTS = 6


def unit_rows(rows):
    fits = [r for r in range(16, LANES + 1, 16) if rows % r == 0]
    return fits[-1] if fits else rows


def rows_to_lanes(column_sums):
    rows = column_sums.shape[0]
    out = []
    for start in range(0, rows, LANES):
        block = column_sums[start : min(start + LANES, rows)]
        if block.shape[0] < LANES:
            fill = jnp.zeros((LANES - block.shape[0], LANES), block.dtype)
            block = jnp.concatenate([block, fill], axis=0)
        out.append(jnp.sum(block.T, axis=0, keepdims=True))
    return jnp.concatenate(out, axis=1) if len(out) > 1 else out[0]


def lanes_to_rows(row, rows):
    out = []
    for start in range(0, rows, LANES):
        block = jnp.broadcast_to(row[:, start : start + LANES], (LANES, LANES)).T
        out.append(block[: min(LANES, rows - start)])
    return jnp.concatenate(out, axis=0) if len(out) > 1 else out[0]


def update_kernel(
    n, ne, r,
    train_ref, other_ref, weight_ref, gain_ref,
    ready_ref, scale_ref, router_ref,
    train_buf, other_buf, stage, part, first, half_sum, far_sum, recip,
    train_sem, other_sem, stage_sem, data_sem,
    small_sem, first_sem, far_sem, recip_sem,
    router_send, router_row_sem, router_col_sem,
):
    experts, _, rows, width = train_ref.shape
    steps = rows // r
    units = experts * steps
    half = n // 2
    me, my_e = lax.axis_index("shard"), lax.axis_index("expert")
    place, side = lax.rem(me, half), lax.div(me, half)

    def shard(d):
        return {"device_id": {"shard": d}, "device_id_type": pl.DeviceIdType.MESH}

    def expert(d):
        return {"device_id": {"expert": d}, "device_id_type": pl.DeviceIdType.MESH}

    def where_is(k):
        start = lax.rem(k, steps) * r
        return lax.div(k, steps), pl.ds(pl.multiple_of(start, 8), r)

    def columns_of(d):
        return pl.ds(pl.multiple_of(d * width, LANES), width)

    def loads(k):
        e, at = where_is(k)
        slot = lax.rem(k, SLOTS)
        return (
            pltpu.make_async_copy(
                train_ref.at[e, :, at, :], train_buf.at[slot], train_sem.at[slot]
            ),
            pltpu.make_async_copy(
                other_ref.at[e, :, at, :], other_buf.at[slot], other_sem.at[slot]
            ),
        )

    def start_loads(k):
        for copy in loads(k):
            copy.start()

    start_loads(0)
    if units > 1:
        start_loads(1)

    mine = columns_of(me)
    router_ref[my_e, :, mine] = (weight_ref[...] * gain_ref[...]).astype(router_ref.dtype)

    barrier = pltpu.get_barrier_semaphore()
    for j in range(1, n):
        pl.semaphore_signal(barrier, inc=1, **shard(lax.rem(me + j, n)))
    for j in range(1, ne):
        pl.semaphore_signal(barrier, inc=1, **expert(lax.rem(my_e + j, ne)))
    pl.semaphore_wait(barrier, n + ne - 2)

    def latest(slot, d):
        return train_buf[slot, d] + other_buf[slot, d].astype(jnp.float32)

    def sum_own(k):
        for copy in loads(k):
            copy.wait()
        slot = lax.rem(k, SLOTS)

        def body(q, carry):
            pair = []
            for t in (0, 1):
                x = latest(slot, t * half + q)
                x = x * x
                total = x[:, :LANES]
                for at in range(LANES, width, LANES):
                    total = total + x[:, at : at + LANES]
                pair.append(rows_to_lanes(total))
            part[k, q] = jnp.concatenate(pair, axis=0)
            return carry

        lax.fori_loop(0, half, body, 0)
        first[k, place] = part[k, place]
        for j in range(1, half):
            q = lax.rem(place + j, half)
            pltpu.make_async_remote_copy(
                src_ref=part.at[k, q],
                dst_ref=first.at[k, place],
                send_sem=small_sem.at[0],
                recv_sem=first_sem.at[k],
                **shard(side * half + q),
            ).start()

    def few(ref, k):
        return ref.at[k, pl.ds(0, half - 1)]

    def sum_half(k):
        pltpu.make_async_remote_copy(
            few(first, k), few(first, k), small_sem.at[0], first_sem.at[k], **shard(me)
        ).wait_recv()
        total = first[k, 0]
        for q in range(1, half):
            total = total + first[k, q]
        half_sum[k] = total
        pltpu.make_async_remote_copy(
            src_ref=half_sum.at[k],
            dst_ref=far_sum.at[k],
            send_sem=small_sem.at[1],
            recv_sem=far_sem.at[k],
            **shard((1 - side) * half + place),
        ).start()

    def sum_all(k):
        pltpu.make_async_remote_copy(
            far_sum.at[k], far_sum.at[k], small_sem.at[1], far_sem.at[k], **shard(me)
        ).wait_recv()
        scale = jnp.sqrt(half_sum[k] + far_sum[k])
        scale_ref[k] = jnp.where(side == 0, scale[0:1], scale[1:2])
        recip[k, place] = 1.0 / scale
        for j in range(1, half):
            q = lax.rem(place + j, half)
            pltpu.make_async_remote_copy(
                src_ref=recip.at[k, place],
                dst_ref=recip.at[k, place],
                send_sem=small_sem.at[2],
                recv_sem=recip_sem.at[k],
                **shard(side * half + q),
            ).start()

    def wait_stage(slot):
        some = stage.at[slot, pl.ds(0, n - 1)]
        pltpu.make_async_remote_copy(
            some, some, stage_sem.at[slot], data_sem.at[0], **shard(me)
        ).wait_send()

    def send(k):
        pltpu.make_async_remote_copy(
            few(recip, k), few(recip, k), small_sem.at[2], recip_sem.at[k], **shard(me)
        ).wait_recv()
        slot, ring = lax.rem(k, SLOTS), lax.rem(k, RING)
        e, at = where_is(k)

        @pl.when(k >= RING)
        def _():
            wait_stage(ring)

        def target(m):
            far = m < half
            t = jnp.where(far, 1 - side, side)
            q = lax.rem(place + jnp.where(far, m, m - half + 1), half)
            return t, q

        def piece(t, q):
            pair = recip[k, q]
            row = jnp.where(t == 0, pair[0:1], pair[1:2])
            factor = lanes_to_rows(row, r)
            factor = jnp.concatenate([factor] * (width // LANES), axis=1)
            return (latest(slot, t * half + q) * factor).astype(stage.dtype)

        def copy_to(m):
            t, q = target(m)
            return pltpu.make_async_remote_copy(
                src_ref=stage.at[ring, m],
                dst_ref=ready_ref.at[e, at, mine],
                send_sem=stage_sem.at[ring],
                recv_sem=data_sem.at[me],
                **shard(t * half + q),
            )

        def body(m, carry):
            stage[ring, m] = piece(*target(m))

            @pl.when(m > 0)
            def _():
                copy_to(m - 1).start()

            return carry

        lax.fori_loop(0, n - 1, body, 0)
        ready_ref[e, at, mine] = piece(side, place)
        copy_to(n - 2).start()

    for j in range(1, n):
        pltpu.make_async_remote_copy(
            src_ref=router_ref.at[my_e, :, mine],
            dst_ref=router_ref.at[my_e, :, mine],
            send_sem=router_send.at[0],
            recv_sem=router_row_sem,
            **shard(lax.rem(me + j, n)),
        ).start()

    def step(i, carry):
        @pl.when(i + 2 < units)
        def _():
            start_loads(i + 2)

        @pl.when(i < units)
        def _():
            sum_own(i)

        @pl.when((i >= 1) & (i < units + 1))
        def _():
            sum_half(i - 1)

        @pl.when((i >= 2) & (i < units + 2))
        def _():
            sum_all(i - 2)

        @pl.when(i >= 3)
        def _():
            send(i - 3)

        return carry

    lax.fori_loop(0, units + 3, step, 0)

    others = router_ref.at[0, :, pl.ds(0, (n - 1) * width)]
    pltpu.make_async_remote_copy(
        others, others, router_send.at[0], router_row_sem, **shard(me)
    ).wait()
    for j in range(1, ne):
        pltpu.make_async_remote_copy(
            src_ref=router_ref.at[my_e],
            dst_ref=router_ref.at[my_e],
            send_sem=router_send.at[1],
            recv_sem=router_col_sem,
            **expert(lax.rem(my_e + j, ne)),
        ).start()

    for slot in range(min(RING, units)):
        wait_stage(slot)
    for j in range(1, n):
        d = lax.rem(me + j, n)
        there = ready_ref.at[:, :, columns_of(d)]
        pltpu.make_async_remote_copy(
            there, there, stage_sem.at[0], data_sem.at[d], **shard(me)
        ).wait_recv()
    sent = part.at[:, pl.ds(0, half - 1)]
    for at in (0, 2):
        pltpu.make_async_remote_copy(
            sent, sent, small_sem.at[at], data_sem.at[0], **shard(me)
        ).wait_send()
    pltpu.make_async_remote_copy(
        half_sum, half_sum, small_sem.at[1], data_sem.at[0], **shard(me)
    ).wait_send()
    others = router_ref.at[pl.ds(0, ne - 1)]
    pltpu.make_async_remote_copy(
        others, others, router_send.at[1], router_col_sem, **shard(me)
    ).wait()


def update(train_down, other_down, weight, gain, n, ne):
    experts, inner, width = train_down.shape
    rows = inner // n
    r = unit_rows(rows)
    units = experts * (rows // r)
    lanes = -(-r // LANES) * LANES
    half = n // 2
    f32, bf16 = jnp.float32, jnp.bfloat16
    dma = pltpu.SemaphoreType.DMA
    return pl.pallas_call(
        functools.partial(update_kernel, n, ne, r),
        out_shape=(
            pltpu.VMEM((experts, rows, width * n), bf16),
            pltpu.VMEM((units, 1, lanes), f32),
            pltpu.VMEM((ne, weight.shape[0], width * n), bf16),
        ),
        in_specs=[
            pl.BlockSpec(memory_space=pl.ANY),
            pl.BlockSpec(memory_space=pl.ANY),
            pl.BlockSpec(memory_space=pltpu.VMEM),
            pl.BlockSpec(memory_space=pltpu.VMEM),
        ],
        out_specs=(pl.BlockSpec(memory_space=pltpu.VMEM),) * 3,
        scratch_shapes=[
            pltpu.VMEM((SLOTS, n, r, width), f32),
            pltpu.VMEM((SLOTS, n, r, width), bf16),
            pltpu.VMEM((RING, n - 1, r, width), bf16),
            pltpu.VMEM((units, half, 2, lanes), f32),
            pltpu.VMEM((units, half, 2, lanes), f32),
            pltpu.VMEM((units, 2, lanes), f32),
            pltpu.VMEM((units, 2, lanes), f32),
            pltpu.VMEM((units, half, 2, lanes), f32),
            dma((SLOTS,)),
            dma((SLOTS,)),
            dma((RING,)),
            dma((n,)),
            dma((3,)),
            dma((units,)),
            dma((units,)),
            dma((units,)),
            dma((2,)),
            dma,
            dma,
        ],
        compiler_params=pltpu.CompilerParams(
            collective_id=0, has_side_effects=True, vmem_limit_bytes=36 * 2**20
        ),
        name="update",
    )(
        train_down.reshape(experts, n, rows, width),
        other_down.reshape(experts, n, rows, width),
        weight,
        gain,
    )


def settle_kernel(
    ready_ref, scale_ref, router_ref, ready_out, scale_out, router_out, ready_sem
):
    copies = [
        pltpu.make_async_copy(ready_ref.at[e], ready_out.at[e], ready_sem.at[e])
        for e in range(ready_ref.shape[0])
    ]
    for copy in copies:
        copy.start()
    scale_out[...] = scale_ref[...]
    router_out[...] = router_ref[...]
    for copy in copies:
        copy.wait()


def settle(ready_down, scale, router):
    vmem = pl.BlockSpec(memory_space=pltpu.VMEM)
    return pl.pallas_call(
        settle_kernel,
        out_shape=tuple(
            jax.ShapeDtypeStruct(x.shape, x.dtype) for x in (ready_down, scale, router)
        ),
        in_specs=[vmem] * 3,
        out_specs=(pl.BlockSpec(memory_space=pl.ANY), vmem, vmem),
        scratch_shapes=[pltpu.SemaphoreType.DMA((ready_down.shape[0],))],
        compiler_params=pltpu.CompilerParams(vmem_limit_bytes=8 * 2**20),
        name="settle",
    )(pltpu.with_memory_space_constraint(ready_down, pltpu.VMEM), scale, router)


def per_device(n, ne, train_down, other_down, router_weight, router_gain):
    experts, inner, width = train_down.shape
    rows = inner // n
    r = unit_rows(rows)
    ready_down, scale, router = update(
        train_down, other_down, router_weight.T, router_gain[None, :], n, ne
    )
    ready_down, scale, router = settle(ready_down, scale, router)
    scale_down = scale.reshape(experts, rows // r, -1)[:, :, :r].reshape(experts, rows)
    serve_router = router.reshape(-1, width * n).T
    return (ready_down, scale_down, serve_router)


def solution(mesh):
    in_specs = (
        P("expert", None, "shard"),
        P("expert", None, "shard"),
        P("shard", "expert"),
        P("shard"),
    )
    out_specs = (P("expert", "shard", None), P("expert", "shard"), P())
    return jax.shard_map(
        functools.partial(per_device, mesh.shape["shard"], mesh.shape["expert"]),
        mesh=mesh,
        in_specs=in_specs,
        out_specs=out_specs,
        check_vma=False,
    )
```

time: 708 us -> 612 us (0.86)
  blocking collectives: 201 us -> 0 us
  Pallas kernels: 428 us -> 608 us
  other arithmetic: 58.6 us -> 0.69 us
  local copies, waits for them, and re-layouts: 19.4 us -> 1.89 us
    all_gather x3 -> x0, blocking collectives: 201 us -> none  [the longest x1 162 us: per_device(): row_router = lax.all_gather(part_router, 'shard', axis=0, tiled=True)]
    pallas_call x1 -> x2, Pallas kernels: 428 us -> 608 us  [the longest x1 599 us: update(): pl.pallas_call(functools.partial(update_kernel, n, ne, r), out_shape=(plt...]
    convert_element_type x2 -> x0, other arithmetic: 34.3 us -> none  [the longest x1 34.3 us: per_device(): (latest_down / jnp.expand_dims(scale_down, 2)).astype(jnp.bfloat16)]
    reduce_sum x2 -> x0, other arithmetic: 24.4 us -> none  [the longest x1 24.2 us: per_device(): part_down = jnp.sum(latest_down * latest_down, axis=2)]
    unnamed x6 -> x0, local copies, waits for them, and re-layouts: 18.6 us -> none
where the time goes in v1:
time: 612 us; the launch traced here: 611 us
  Pallas kernels  608 us (99%)
    pallas_call x1, Pallas kernels, update(): pl.pallas_call(functools.partial(update_kernel, n, ne, r), out_shape=(plt...  599 us

profile of v1, /device:TPU:0, one launch (start us, length us, event | category | flops | bytes accessed | tf_op | source)
XLA Modules:
  0.0 611.5 jit_solution(15739560702051971674)
XLA Ops:
  0.6 599.3 %update.1 = (bf16[4,800,4096]{2,1,0:T(8,128)(2,1)S(1)}, f32[40,1,128]{2,1,0:T(1,128)S(1)}, bf16[4,4,4096]{2,1,0:T(4,128)(2,1)S(1)}) custom-call(f32[4,8,800,512]{3,2,1,0:T(8,128)} %bitcast.7, bf16[4,8,800,512]{3,2,1,0:T(8,128)(2,1)} %bitcast.8, f32[4,512]{1,0:T(4,128)} %bitcast.11, f32[1,512]{1,0:T(1,128)} %bitcast.12), custom_call_target="tpu_custom_call" | custom-call | tf_op jit(solution)/shard_map/update/pallas_call | solution.py:298
  599.9 8.9 %settle.1 = (bf16[4,800,4096]{2,1,0:T(8,128)(2,1)}, f32[40,1,128]{2,1,0:T(1,128)S(1)}, bf16[4,4,4096]{2,1,0:T(4,128)(2,1)S(1)}) custom-call(bf16[4,800,4096]{2,1,0:T(8,128)(2,1)S(1)} %get-tuple-element.9.ready_ref, f32[40,1,128]{2,1,0:T(1,128)S(1)} %get-tuple-element.10.scale_ref, bf16[4,4,4096]{2,1,0:T(4,128)(2,1)S(1)} %get-tuple-element.11.router_ref), custom_call_target="tpu_custom_call" | custom-call | tf_op jit(solution)/shard_map/settle/pallas_call | solution.py:362
  608.9 0.7 reshape.25
  609.6 0.5 broadcast.3
  610.1 0.7 reduce.3
  610.8 0.7 reshape.24
  (1 shorter events, 0.0 us)

commit v2 on v1

v2 whole, which is shorter than its diff:
```python
import functools

import jax
import jax.numpy as jnp
from jax import lax
from jax.experimental import pallas as pl
from jax.experimental.pallas import tpu as pltpu
from jax.sharding import PartitionSpec as P

LANES = 128
UNIT = 128
RING = 4
GROUP = 4
LAGS = (7, 4, 2)


def unit_rows(rows):
    fits = [r for r in range(16, UNIT + 1, 16) if rows % r == 0]
    return fits[-1] if fits else rows


def rows_to_lanes(column_sums):
    rows = column_sums.shape[0]
    out = []
    for start in range(0, rows, LANES):
        block = column_sums[start : min(start + LANES, rows)]
        if block.shape[0] < LANES:
            fill = jnp.zeros((LANES - block.shape[0], LANES), block.dtype)
            block = jnp.concatenate([block, fill], axis=0)
        out.append(jnp.sum(block.T, axis=0, keepdims=True))
    return jnp.concatenate(out, axis=1) if len(out) > 1 else out[0]


def lanes_to_rows(row, rows):
    out = []
    for start in range(0, rows, LANES):
        block = jnp.broadcast_to(row[:, start : start + LANES], (LANES, LANES)).T
        out.append(block[: min(LANES, rows - start)])
    return jnp.concatenate(out, axis=0) if len(out) > 1 else out[0]


def update_kernel(
    n, ne, r, head,
    train_ref, other_ref, weight_ref, gain_ref,
    ready_ref, scale_ref, router_ref,
    train_buf, other_buf, stage, part, direct, first, half_sum, far_sum, recip,
    train_sem, other_sem, stage_sem, data_sem,
    small_sem, direct_sem, first_sem, far_sem, recip_sem,
    router_send, router_row_sem, router_col_sem,
):
    experts, _, rows, width = train_ref.shape
    steps = rows // r
    units = experts * steps
    groups = (units - head) // GROUP
    half = n // 2
    me, my_e = lax.axis_index("shard"), lax.axis_index("expert")
    place, side = lax.rem(me, half), lax.div(me, half)

    def shard(d):
        return {"device_id": {"shard": d}, "device_id_type": pl.DeviceIdType.MESH}

    def expert(d):
        return {"device_id": {"expert": d}, "device_id_type": pl.DeviceIdType.MESH}

    def wait_recv(ref, sem):
        pltpu.make_async_remote_copy(ref, ref, small_sem.at[0], sem, **shard(me)).wait_recv()

    def wait_send(ref, sem):
        pltpu.make_async_remote_copy(ref, ref, sem, data_sem.at[0], **shard(me)).wait_send()

    def where_is(k):
        start = lax.rem(k, steps) * r
        return lax.div(k, steps), pl.ds(pl.multiple_of(start, 8), r)

    def columns_of(d):
        return pl.ds(pl.multiple_of(d * width, LANES), width)

    def loads(k, slot):
        e, at = where_is(k)
        return (
            pltpu.make_async_copy(
                train_ref.at[e, :, at, :], train_buf.at[slot], train_sem.at[slot]
            ),
            pltpu.make_async_copy(
                other_ref.at[e, :, at, :], other_buf.at[slot], other_sem.at[slot]
            ),
        )

    def start_loads(k, slot):
        for copy in loads(k, slot):
            copy.start()

    def wait_loads(k, slot):
        for copy in loads(k, slot):
            copy.wait()

    def sum_slot(k):
        return lax.rem(k, GROUP)

    def send_slot(k):
        return GROUP + lax.rem(k, 3)

    start_loads(0, 0)
    if units > 1:
        start_loads(1, 1)

    mine = columns_of(me)
    router_ref[my_e, :, mine] = (weight_ref[...] * gain_ref[...]).astype(router_ref.dtype)

    barrier = pltpu.get_barrier_semaphore()
    for j in range(1, n):
        pl.semaphore_signal(barrier, inc=1, **shard(lax.rem(me + j, n)))
    for j in range(1, ne):
        pl.semaphore_signal(barrier, inc=1, **expert(lax.rem(my_e + j, ne)))
    pl.semaphore_wait(barrier, n + ne - 2)

    def latest(slot, d):
        return train_buf[slot, d] + other_buf[slot, d].astype(jnp.float32)

    def sum_own(k):
        slot = sum_slot(k)
        wait_loads(k, slot)

        def body(q, carry):
            pair = []
            for t in (0, 1):
                x = latest(slot, t * half + q)
                x = x * x
                total = x[:, :LANES]
                for at in range(LANES, width, LANES):
                    total = total + x[:, at : at + LANES]
                pair.append(rows_to_lanes(total))
            part[q, k] = jnp.concatenate(pair, axis=0)
            return carry

        lax.fori_loop(0, half, body, 0)

    def own_side(pair):
        return jnp.where(side == 0, pair[..., 0:1, :], pair[..., 1:2, :])

    def send_direct(k):
        for q in range(half):
            direct[k, me, q] = part[q, k]
        for j in range(1, n):
            pltpu.make_async_remote_copy(
                src_ref=part.at[:, k],
                dst_ref=direct.at[k, me],
                send_sem=small_sem.at[3],
                recv_sem=direct_sem.at[k],
                **shard(lax.rem(me + (half + j - 1 if j <= half else j - half), n)),
            ).start()

    def sum_direct(k):
        wait_recv(direct.at[k, pl.ds(0, n - 1)], direct_sem.at[k])
        for q in range(half):
            total = direct[k, 0, q]
            for s in range(1, n):
                total = total + direct[k, s, q]
            scale = jnp.sqrt(total)
            recip[q, k] = 1.0 / scale

            @pl.when(place == q)
            def _(scale=scale):
                scale_ref[k] = own_side(scale)

    def units_of(g):
        return pl.ds(head + g * GROUP, GROUP)

    def sum_group(g):
        at = units_of(g)

        def body(j, carry):
            k = head + g * GROUP + j
            sum_own(k)

            @pl.when(k + GROUP < units)
            def _():
                start_loads(k + GROUP, sum_slot(k))

            return carry

        lax.fori_loop(0, GROUP, body, 0)
        first[place, at] = part[place, at]
        for j in range(1, half):
            q = lax.rem(place + j, half)
            pltpu.make_async_remote_copy(
                src_ref=part.at[q, at],
                dst_ref=first.at[place, at],
                send_sem=small_sem.at[0],
                recv_sem=first_sem.at[g],
                **shard(side * half + q),
            ).start()

    def sum_half(g):
        at = units_of(g)
        wait_recv(first.at[pl.ds(0, half - 1), at], first_sem.at[g])
        total = first[0, at]
        for q in range(1, half):
            total = total + first[q, at]
        half_sum[at] = total
        pltpu.make_async_remote_copy(
            src_ref=half_sum.at[at],
            dst_ref=far_sum.at[at],
            send_sem=small_sem.at[1],
            recv_sem=far_sem.at[g],
            **shard((1 - side) * half + place),
        ).start()

    def sum_all(g):
        at = units_of(g)
        wait_recv(far_sum.at[at], far_sem.at[g])
        scale = jnp.sqrt(half_sum[at] + far_sum[at])
        scale_ref[at] = own_side(scale)
        recip[place, at] = 1.0 / scale
        for j in range(1, half):
            q = lax.rem(place + j, half)
            pltpu.make_async_remote_copy(
                src_ref=recip.at[place, at],
                dst_ref=recip.at[place, at],
                send_sem=small_sem.at[2],
                recv_sem=recip_sem.at[g],
                **shard(side * half + q),
            ).start()

    def wait_stage(slot):
        wait_send(stage.at[slot, pl.ds(0, n - 1)], stage_sem.at[slot])

    def send(k):
        slot, ring = send_slot(k), lax.rem(k, RING)
        e, at = where_is(k)
        wait_loads(k, slot)

        @pl.when(k >= RING)
        def _():
            wait_stage(ring)

        def target(m):
            m = lax.rem(m + jnp.where(k == 0, 0, half), n - 1)
            far = m < half
            t = jnp.where(far, 1 - side, side)
            q = lax.rem(place + jnp.where(far, m, m - half + 1), half)
            return t, q

        def piece(t, q):
            pair = recip[q, k]
            row = jnp.where(t == 0, pair[0:1], pair[1:2])
            factor = lanes_to_rows(row, r)
            factor = jnp.concatenate([factor] * (width // LANES), axis=1)
            return (latest(slot, t * half + q) * factor).astype(stage.dtype)

        def copy_to(m):
            t, q = target(m)
            return pltpu.make_async_remote_copy(
                src_ref=stage.at[ring, m],
                dst_ref=ready_ref.at[e, at, mine],
                send_sem=stage_sem.at[ring],
                recv_sem=data_sem.at[me],
                **shard(t * half + q),
            )

        def body(m, carry):
            stage[ring, m] = piece(*target(m))

            @pl.when(m > 0)
            def _():
                copy_to(m - 1).start()

            return carry

        lax.fori_loop(0, n - 1, body, 0)
        ready_ref[e, at, mine] = piece(side, place)
        copy_to(n - 2).start()

    for k in range(head):
        sum_own(k)
        send_direct(k)
        if k < min(3, units):
            start_loads(k, send_slot(k))
        if k + 2 < min(GROUP, units):
            start_loads(k + 2, k + 2)
        if k + GROUP < head:
            start_loads(k + GROUP, k)
    for k in range(head, min(head + GROUP, units)):
        start_loads(k, sum_slot(k))

    def step(i, carry):
        def at_lag(lag, start):
            g = jnp.where(i == start, 0, lax.div(i + lag - head, GROUP))
            due = (i == start) | (
                (i + lag >= head + GROUP) & (lax.rem(i + lag - head, GROUP) == 0)
            )
            return g, due & (g < groups)

        if groups > 0:
            g, due = at_lag(LAGS[2], 3)

            @pl.when(due)
            def _():
                sum_all(g)

            g, due = at_lag(LAGS[1], 2)

            @pl.when(due)
            def _():
                sum_half(g)

        @pl.when(i < head)
        def _():
            sum_direct(i)

        if groups > 0:

            @pl.when((i >= head) & (lax.rem(i - head, GROUP) == 0))
            def _():
                g = lax.div(i - head, GROUP)
                wait_recv(recip.at[pl.ds(0, half - 1), units_of(g)], recip_sem.at[g])

        send(i)

        @pl.when(i + 3 < units)
        def _():
            start_loads(i + 3, send_slot(i))

        if groups > 0:
            g, due = at_lag(LAGS[0], 0)

            @pl.when(due)
            def _():
                sum_group(g)

        return carry

    def send_router():
        for j in range(1, n):
            pltpu.make_async_remote_copy(
                src_ref=router_ref.at[my_e, :, mine],
                dst_ref=router_ref.at[my_e, :, mine],
                send_sem=router_send.at[0],
                recv_sem=router_row_sem,
                **shard(lax.rem(me + j, n)),
            ).start()

    lax.fori_loop(0, 1, step, 0)
    send_router()
    lax.fori_loop(1, units, step, 0)

    others = router_ref.at[0, :, pl.ds(0, (n - 1) * width)]
    pltpu.make_async_remote_copy(
        others, others, router_send.at[0], router_row_sem, **shard(me)
    ).wait()
    for j in range(1, ne):
        pltpu.make_async_remote_copy(
            src_ref=router_ref.at[my_e],
            dst_ref=router_ref.at[my_e],
            send_sem=router_send.at[1],
            recv_sem=router_col_sem,
            **expert(lax.rem(my_e + j, ne)),
        ).start()

    for slot in range(min(RING, units)):
        wait_stage(slot)
    wait_send(direct.at[:, pl.ds(0, n - 1)], small_sem.at[3])
    if groups > 0:
        late = pl.ds(head, groups * GROUP)
        wait_send(part.at[pl.ds(0, half - 1), late], small_sem.at[0])
        wait_send(half_sum.at[late], small_sem.at[1])
        wait_send(recip.at[pl.ds(0, half - 1), late], small_sem.at[2])
    others = router_ref.at[pl.ds(0, ne - 1)]
    pltpu.make_async_remote_copy(
        others, others, router_send.at[1], router_col_sem, **shard(me)
    ).wait()
    for j in range(1, n):
        d = lax.rem(me + j, n)
        wait_recv(ready_ref.at[:, :, columns_of(d)], data_sem.at[d])


def update(train_down, other_down, weight, gain, n, ne):
    experts, inner, width = train_down.shape
    rows = inner // n
    r = unit_rows(rows)
    units = experts * (rows // r)
    lanes = -(-r // LANES) * LANES
    half = n // 2
    head = units if units <= GROUP else GROUP + units % GROUP
    groups = max(1, (units - head) // GROUP)
    result_bytes = 2 * experts * rows * width * n
    f32, bf16 = jnp.float32, jnp.bfloat16
    dma = pltpu.SemaphoreType.DMA
    return pl.pallas_call(
        functools.partial(update_kernel, n, ne, r, head),
        out_shape=(
            pltpu.VMEM((experts, rows, width * n), bf16),
            pltpu.VMEM((units, 1, lanes), f32),
            pltpu.VMEM((ne, weight.shape[0], width * n), bf16),
        ),
        in_specs=[
            pl.BlockSpec(memory_space=pl.ANY),
            pl.BlockSpec(memory_space=pl.ANY),
            pl.BlockSpec(memory_space=pltpu.VMEM),
            pl.BlockSpec(memory_space=pltpu.VMEM),
        ],
        out_specs=(pl.BlockSpec(memory_space=pltpu.VMEM),) * 3,
        scratch_shapes=[
            pltpu.VMEM((GROUP + 3, n, r, width), f32),
            pltpu.VMEM((GROUP + 3, n, r, width), bf16),
            pltpu.VMEM((RING, n - 1, r, width), bf16),
            pltpu.VMEM((half, units, 2, lanes), f32),
            pltpu.VMEM((head, n, half, 2, lanes), f32),
            pltpu.VMEM((half, units, 2, lanes), f32),
            pltpu.VMEM((units, 2, lanes), f32),
            pltpu.VMEM((units, 2, lanes), f32),
            pltpu.VMEM((half, units, 2, lanes), f32),
            dma((GROUP + 3,)),
            dma((GROUP + 3,)),
            dma((RING,)),
            dma((n,)),
            dma((4,)),
            dma((head,)),
            dma((groups,)),
            dma((groups,)),
            dma((groups,)),
            dma((2,)),
            dma,
            dma,
        ],
        compiler_params=pltpu.CompilerParams(
            collective_id=0,
            has_side_effects=True,
            vmem_limit_bytes=62 * 2**20 - result_bytes,
        ),
        name="update",
    )(
        train_down.reshape(experts, n, rows, width),
        other_down.reshape(experts, n, rows, width),
        weight,
        gain,
    )


def settle_kernel(
    ready_ref, scale_ref, router_ref, ready_out, scale_out, router_out, ready_sem
):
    experts, rows = scale_out.shape
    copies = [
        pltpu.make_async_copy(ready_ref.at[e], ready_out.at[e], ready_sem.at[e])
        for e in range(experts)
    ]
    for copy in copies:
        copy.start()
    steps = scale_ref.shape[0] // experts
    r = rows // steps
    for e in range(experts):
        runs = [scale_ref[e * steps + j][:, :r] for j in range(steps)]
        scale_out[e : e + 1, :] = jnp.concatenate(runs, axis=1)
    groups = [router_ref[g].astype(jnp.float32) for g in range(router_ref.shape[0])]
    router_out[...] = jnp.concatenate(groups, axis=0).astype(router_out.dtype)
    for copy in copies:
        copy.wait()


def settle(ready_down, scale, router):
    vmem = pl.BlockSpec(memory_space=pltpu.VMEM)
    experts, rows, width = ready_down.shape
    return pl.pallas_call(
        settle_kernel,
        out_shape=(
            jax.ShapeDtypeStruct(ready_down.shape, ready_down.dtype),
            jax.ShapeDtypeStruct((experts, rows), scale.dtype),
            jax.ShapeDtypeStruct((router.shape[0] * router.shape[1], width), router.dtype),
        ),
        in_specs=[vmem] * 3,
        out_specs=(pl.BlockSpec(memory_space=pl.ANY), vmem, vmem),
        scratch_shapes=[pltpu.SemaphoreType.DMA((experts,))],
        compiler_params=pltpu.CompilerParams(vmem_limit_bytes=8 * 2**20),
        name="settle",
    )(pltpu.with_memory_space_constraint(ready_down, pltpu.VMEM), scale, router)


def per_device(n, ne, train_down, other_down, router_weight, router_gain):
    ready_down, scale, router = update(
        train_down, other_down, router_weight.T, router_gain[None, :], n, ne
    )
    ready_down, scale_down, router = settle(ready_down, scale, router)
    return (ready_down, scale_down, router.T)


def solution(mesh):
    in_specs = (
        P("expert", None, "shard"),
        P("expert", None, "shard"),
        P("shard", "expert"),
        P("shard"),
    )
    out_specs = (P("expert", "shard", None), P("expert", "shard"), P())
    return jax.shard_map(
        functools.partial(per_device, mesh.shape["shard"], mesh.shape["expert"]),
        mesh=mesh,
        in_specs=in_specs,
        out_specs=out_specs,
        check_vma=False,
    )
```

time: 612 us -> 590 us (0.964)
  Pallas kernels: 608 us -> 589 us
    pallas_call x2, Pallas kernels: 608 us -> 589 us  [the longest x1 579 us: update(): pl.pallas_call(functools.partial(update_kernel, n, ne, r, head), out_shap...]
where the time goes in v2:
time: 590 us
  Pallas kernels  589 us (100%)
    pallas_call x1, Pallas kernels, update(): pl.pallas_call(functools.partial(update_kernel, n, ne, r, head), out_shap...  579 us

profile of v2, /device:TPU:0, one launch (start us, length us, event | category | flops | bytes accessed | tf_op | source)
XLA Modules:
  0.0 589.5 jit_solution(1369319963154471178)
XLA Ops:
  0.6 579.3 %update.1 = (bf16[4,800,4096]{2,1,0:T(8,128)(2,1)S(1)}, f32[40,1,128]{2,1,0:T(1,128)S(1)}, bf16[4,4,4096]{2,1,0:T(4,128)(2,1)S(1)}) custom-call(f32[4,8,800,512]{3,2,1,0:T(8,128)} %bitcast.5, bf16[4,8,800,512]{3,2,1,0:T(8,128)(2,1)} %bitcast.6, f32[4,512]{1,0:T(4,128)} %bitcast.7, f32[1,512]{1,0:T(1,128)} %bitcast.8), custom_call_target="tpu_custom_call" | custom-call | tf_op jit(solution)/shard_map/update/pallas_call | solution.py:389
  579.9 9.6 %settle.1 = (bf16[4,800,4096]{2,1,0:T(8,128)(2,1)}, f32[4,800]{1,0:T(4,128)}, bf16[16,4096]{1,0:T(8,128)(2,1)}) custom-call(bf16[4,800,4096]{2,1,0:T(8,128)(2,1)S(1)} %get-tuple-element.9.ready_ref, f32[40,1,128]{2,1,0:T(1,128)S(1)} %get-tuple-element.10.scale_ref, bf16[4,4,4096]{2,1,0:T(4,128)(2,1)S(1)} %get-tuple-element.11.router_ref), custom_call_target="tpu_custom_call" | custom-call | tf_op jit(solution)/shard_map/settle/pallas_call | solution.py:464

commit v3 on v2

--- a/solution.py
+++ b/solution.py
@@ -10,13 +10,20 @@
 LANES = 128
 UNIT = 128
 RING = 4
-GROUP = 4
+HEAD = 4
+GROUP = 12
 LAGS = (7, 4, 2)
 
 
 def unit_rows(rows):
     fits = [r for r in range(16, UNIT + 1, 16) if rows % r == 0]
     return fits[-1] if fits else rows
+
+
+def units_apart(units):
+    head = min(HEAD, units)
+    fits = [g for g in range(HEAD, GROUP + 1) if (units - head) % g == 0]
+    return (head, fits[-1]) if fits else (units, 1)
 
 
 def rows_to_lanes(column_sums):
@@ -40,9 +47,9 @@
 
 
 def update_kernel(
-    n, ne, r, head,
+    n, ne, r, head, group, late,
     train_ref, other_ref, weight_ref, gain_ref,
-    ready_ref, scale_ref, router_ref,
+    ready_ref, scale_ref, router_ref, late_ref,
     train_buf, other_buf, stage, part, direct, first, half_sum, far_sum, recip,
     train_sem, other_sem, stage_sem, data_sem,
     small_sem, direct_sem, first_sem, far_sem, recip_sem,
@@ -51,8 +58,9 @@
     experts, _, rows, width = train_ref.shape
     steps = rows // r
     units = experts * steps
-    groups = (units - head) // GROUP
+    groups = (units - head) // group
     half = n // 2
+    ring_size = stage.shape[0]
     me, my_e = lax.axis_index("shard"), lax.axis_index("expert")
     place, side = lax.rem(me, half), lax.div(me, half)
 
@@ -94,11 +102,11 @@
         for copy in loads(k, slot):
             copy.wait()
 
-    def sum_slot(k):
-        return lax.rem(k, GROUP)
-
-    def send_slot(k):
-        return GROUP + lax.rem(k, 3)
+    def slot_of(k):
+        return lax.rem(k, HEAD)
+
+    def ahead_slot(k):
+        return HEAD + lax.rem(k, HEAD)
 
     start_loads(0, 0)
     if units > 1:
@@ -117,8 +125,7 @@
     def latest(slot, d):
         return train_buf[slot, d] + other_buf[slot, d].astype(jnp.float32)
 
-    def sum_own(k):
-        slot = sum_slot(k)
+    def sum_own(k, slot):
         wait_loads(k, slot)
 
         def body(q, carry):
@@ -164,22 +171,22 @@
                 scale_ref[k] = own_side(scale)
 
     def units_of(g):
-        return pl.ds(head + g * GROUP, GROUP)
+        return pl.ds(head + g * group, group)
 
     def sum_group(g):
         at = units_of(g)
 
         def body(j, carry):
-            k = head + g * GROUP + j
-            sum_own(k)
-
-            @pl.when(k + GROUP < units)
+            k = head + g * group + j
+            sum_own(k, ahead_slot(k))
+
+            @pl.when(k + HEAD < units)
             def _():
-                start_loads(k + GROUP, sum_slot(k))
+                start_loads(k + HEAD, ahead_slot(k))
 
             return carry
 
-        lax.fori_loop(0, GROUP, body, 0)
+        lax.fori_loop(0, group, body, 0)
         first[place, at] = part[place, at]
         for j in range(1, half):
             q = lax.rem(place + j, half)
@@ -226,16 +233,22 @@
         wait_send(stage.at[slot, pl.ds(0, n - 1)], stage_sem.at[slot])
 
     def send(k):
-        slot, ring = send_slot(k), lax.rem(k, RING)
+        slot, ring = slot_of(k), lax.rem(k, ring_size)
         e, at = where_is(k)
-        wait_loads(k, slot)
-
-        @pl.when(k >= RING)
+
+        @pl.when(k >= head)
+        def _():
+            wait_loads(k, slot)
+
+        @pl.when(k >= ring_size)
         def _():
             wait_stage(ring)
 
+        is_late = k >= units - late
+
         def target(m):
-            m = lax.rem(m + jnp.where(k == 0, 0, half), n - 1)
+            swapped = jnp.where(m < half, m + half - 1, m - half + 1)
+            m = jnp.where(is_late & (m > 0), swapped, m)
             far = m < half
             t = jnp.where(far, 1 - side, side)
             q = lax.rem(place + jnp.where(far, m, m - half + 1), half)
@@ -258,36 +271,40 @@
                 **shard(t * half + q),
             )
 
+        @pl.when(is_late)
+        def _():
+            late_ref[k - (units - late)] = piece(*target(0))
+
+        start = jnp.where(is_late, 1, 0)
+
         def body(m, carry):
             stage[ring, m] = piece(*target(m))
 
-            @pl.when(m > 0)
+            @pl.when(m > start)
             def _():
                 copy_to(m - 1).start()
 
             return carry
 
-        lax.fori_loop(0, n - 1, body, 0)
+        lax.fori_loop(start, n - 1, body, 0)
         ready_ref[e, at, mine] = piece(side, place)
         copy_to(n - 2).start()
 
+    for k in range(2, min(HEAD, units)):
+        start_loads(k, k)
     for k in range(head):
-        sum_own(k)
+        sum_own(k, slot_of(k))
         send_direct(k)
-        if k < min(3, units):
-            start_loads(k, send_slot(k))
-        if k + 2 < min(GROUP, units):
-            start_loads(k + 2, k + 2)
-        if k + GROUP < head:
-            start_loads(k + GROUP, k)
-    for k in range(head, min(head + GROUP, units)):
-        start_loads(k, sum_slot(k))
+        if k + HEAD < head:
+            start_loads(k + HEAD, k)
+    for k in range(head, min(head + HEAD, units)):
+        start_loads(k, ahead_slot(k))
 
     def step(i, carry):
         def at_lag(lag, start):
-            g = jnp.where(i == start, 0, lax.div(i + lag - head, GROUP))
+            g = jnp.where(i == start, 0, lax.div(i + lag - head, group))
             due = (i == start) | (
-                (i + lag >= head + GROUP) & (lax.rem(i + lag - head, GROUP) == 0)
+                (i + lag >= head + group) & (lax.rem(i + lag - head, group) == 0)
             )
             return g, due & (g < groups)
 
@@ -310,16 +327,16 @@
 
         if groups > 0:
 
-            @pl.when((i >= head) & (lax.rem(i - head, GROUP) == 0))
+            @pl.when((i >= head) & (lax.rem(i - head, group) == 0))
             def _():
-                g = lax.div(i - head, GROUP)
+                g = lax.div(i - head, group)
                 wait_recv(recip.at[pl.ds(0, half - 1), units_of(g)], recip_sem.at[g])
 
         send(i)
 
-        @pl.when(i + 3 < units)
+        @pl.when((i + HEAD >= head) & (i + HEAD < units))
         def _():
-            start_loads(i + 3, send_slot(i))
+            start_loads(i + HEAD, slot_of(i))
 
         if groups > 0:
             g, due = at_lag(LAGS[0], 0)
@@ -357,21 +374,29 @@
             **expert(lax.rem(my_e + j, ne)),
         ).start()
 
-    for slot in range(min(RING, units)):
-        wait_stage(slot)
+    for k in range(max(0, units - ring_size), units):
+        if k < units - late:
+            wait_stage(k % ring_size)
+        else:
+            wait_send(stage.at[k % ring_size, pl.ds(1, n - 2)], stage_sem.at[k % ring_size])
     wait_send(direct.at[:, pl.ds(0, n - 1)], small_sem.at[3])
     if groups > 0:
-        late = pl.ds(head, groups * GROUP)
-        wait_send(part.at[pl.ds(0, half - 1), late], small_sem.at[0])
-        wait_send(half_sum.at[late], small_sem.at[1])
-        wait_send(recip.at[pl.ds(0, half - 1), late], small_sem.at[2])
+        grouped = pl.ds(head, groups * group)
+        wait_send(part.at[pl.ds(0, half - 1), grouped], small_sem.at[0])
+        wait_send(half_sum.at[grouped], small_sem.at[1])
+        wait_send(recip.at[pl.ds(0, half - 1), grouped], small_sem.at[2])
     others = router_ref.at[pl.ds(0, ne - 1)]
     pltpu.make_async_remote_copy(
         others, others, router_send.at[1], router_col_sem, **shard(me)
     ).wait()
     for j in range(1, n):
         d = lax.rem(me + j, n)
-        wait_recv(ready_ref.at[:, :, columns_of(d)], data_sem.at[d])
+        if j != half:
+            wait_recv(ready_ref.at[:, :, columns_of(d)], data_sem.at[d])
+            continue
+        early = rows - late // experts * r
+        if early > 0:
+            wait_recv(ready_ref.at[:, pl.ds(0, early), columns_of(d)], data_sem.at[d])
 
 
 def update(train_down, other_down, weight, gain, n, ne):
@@ -381,17 +406,20 @@
     units = experts * (rows // r)
     lanes = -(-r // LANES) * LANES
     half = n // 2
-    head = units if units <= GROUP else GROUP + units % GROUP
-    groups = max(1, (units - head) // GROUP)
+    head, group = units_apart(units)
+    groups = max(1, (units - head) // group)
+    late = experts
+    ring_size = max(RING, late)
     result_bytes = 2 * experts * rows * width * n
     f32, bf16 = jnp.float32, jnp.bfloat16
     dma = pltpu.SemaphoreType.DMA
     return pl.pallas_call(
-        functools.partial(update_kernel, n, ne, r, head),
+        functools.partial(update_kernel, n, ne, r, head, group, late),
         out_shape=(
             pltpu.VMEM((experts, rows, width * n), bf16),
             pltpu.VMEM((units, 1, lanes), f32),
             pltpu.VMEM((ne, weight.shape[0], width * n), bf16),
+            pltpu.VMEM((late, r, width), bf16),
         ),
         in_specs=[
             pl.BlockSpec(memory_space=pl.ANY),
@@ -399,20 +427,20 @@
             pl.BlockSpec(memory_space=pltpu.VMEM),
             pl.BlockSpec(memory_space=pltpu.VMEM),
         ],
-        out_specs=(pl.BlockSpec(memory_space=pltpu.VMEM),) * 3,
+        out_specs=(pl.BlockSpec(memory_space=pltpu.VMEM),) * 4,
         scratch_shapes=[
-            pltpu.VMEM((GROUP + 3, n, r, width), f32),
-            pltpu.VMEM((GROUP + 3, n, r, width), bf16),
-            pltpu.VMEM((RING, n - 1, r, width), bf16),
+            pltpu.VMEM((2 * HEAD, n, r, width), f32),
+            pltpu.VMEM((2 * HEAD, n, r, width), bf16),
+            pltpu.VMEM((ring_size, n - 1, r, width), bf16),
             pltpu.VMEM((half, units, 2, lanes), f32),
             pltpu.VMEM((head, n, half, 2, lanes), f32),
             pltpu.VMEM((half, units, 2, lanes), f32),
             pltpu.VMEM((units, 2, lanes), f32),
             pltpu.VMEM((units, 2, lanes), f32),
             pltpu.VMEM((half, units, 2, lanes), f32),
-            dma((GROUP + 3,)),
-            dma((GROUP + 3,)),
-            dma((RING,)),
+            dma((2 * HEAD,)),
+            dma((2 * HEAD,)),
+            dma((ring_size,)),
             dma((n,)),
             dma((4,)),
             dma((head,)),
@@ -438,49 +466,97 @@
 
 
 def settle_kernel(
-    ready_ref, scale_ref, router_ref, ready_out, scale_out, router_out, ready_sem
+    ready_ref, scale_ref, router_ref, ready_out, scale_out, router_out,
+    scale_buf, router_buf, ready_sem, small_sem,
 ):
-    experts, rows = scale_out.shape
+    experts, rows = scale_buf.shape
+    steps = scale_ref.shape[0] // experts
+    r = rows // steps
     copies = [
-        pltpu.make_async_copy(ready_ref.at[e], ready_out.at[e], ready_sem.at[e])
+        pltpu.make_async_copy(
+            ready_ref.at[e, pl.ds(j * r, r)], ready_out.at[e, pl.ds(j * r, r)], ready_sem.at[e]
+        )
         for e in range(experts)
+        for j in range(steps)
     ]
     for copy in copies:
         copy.start()
-    steps = scale_ref.shape[0] // experts
-    r = rows // steps
     for e in range(experts):
         runs = [scale_ref[e * steps + j][:, :r] for j in range(steps)]
-        scale_out[e : e + 1, :] = jnp.concatenate(runs, axis=1)
+        scale_buf[e : e + 1, :] = jnp.concatenate(runs, axis=1)
     groups = [router_ref[g].astype(jnp.float32) for g in range(router_ref.shape[0])]
-    router_out[...] = jnp.concatenate(groups, axis=0).astype(router_out.dtype)
+    router_buf[...] = jnp.concatenate(groups, axis=0).astype(router_buf.dtype)
+    small = [
+        pltpu.make_async_copy(scale_buf, scale_out, small_sem.at[0]),
+        pltpu.make_async_copy(router_buf, router_out, small_sem.at[1]),
+    ]
+    for copy in small:
+        copy.start()
+    for copy in small + copies:
+        copy.wait()
+
+
+def settle(ready_down, scale, router):
+    vmem, hbm = pl.BlockSpec(memory_space=pltpu.VMEM), pl.BlockSpec(memory_space=pl.ANY)
+    experts, rows, width = ready_down.shape
+    small = [
+        ((experts, rows), scale.dtype),
+        ((router.shape[0] * router.shape[1], width), router.dtype),
+    ]
+    return pl.pallas_call(
+        settle_kernel,
+        out_shape=(jax.ShapeDtypeStruct(ready_down.shape, ready_down.dtype),)
+        + tuple(jax.ShapeDtypeStruct(*x) for x in small),
+        in_specs=[vmem] * 3,
+        out_specs=(hbm,) * 3,
+        scratch_shapes=[pltpu.VMEM(*x) for x in small]
+        + [pltpu.SemaphoreType.DMA((experts,)), pltpu.SemaphoreType.DMA((2,))],
+        compiler_params=pltpu.CompilerParams(vmem_limit_bytes=8 * 2**20),
+        cost_estimate=pl.CostEstimate(
+            flops=10**8, bytes_accessed=2 * ready_down.size, transcendentals=0
+        ),
+        name="settle",
+    )(pltpu.with_memory_space_constraint(ready_down, pltpu.VMEM), scale, router)
+
+
+def place_late_kernel(n, late_ref, _, ready_ref, sem):
+    late, r, width = late_ref.shape
+    experts, rows, _ = ready_ref.shape
+    steps = rows // r
+    far = lax.rem(lax.axis_index("shard") + n // 2, n)
+    columns = pl.ds(pl.multiple_of(far * width, LANES), width)
+    copies = []
+    for j in range(late):
+        e, at = divmod(experts * steps - late + j, steps)
+        there = ready_ref.at[e, pl.ds(at * r, r), columns]
+        copies.append(pltpu.make_async_copy(late_ref.at[j], there, sem.at[j]))
+    for copy in copies:
+        copy.start()
     for copy in copies:
         copy.wait()
 
 
-def settle(ready_down, scale, router):
-    vmem = pl.BlockSpec(memory_space=pltpu.VMEM)
-    experts, rows, width = ready_down.shape
+def place_late(late_down, ready_down, n):
+    hbm = pl.BlockSpec(memory_space=pl.ANY)
     return pl.pallas_call(
-        settle_kernel,
-        out_shape=(
-            jax.ShapeDtypeStruct(ready_down.shape, ready_down.dtype),
-            jax.ShapeDtypeStruct((experts, rows), scale.dtype),
-            jax.ShapeDtypeStruct((router.shape[0] * router.shape[1], width), router.dtype),
-        ),
-        in_specs=[vmem] * 3,
-        out_specs=(pl.BlockSpec(memory_space=pl.ANY), vmem, vmem),
-        scratch_shapes=[pltpu.SemaphoreType.DMA((experts,))],
+        functools.partial(place_late_kernel, n),
+        out_shape=jax.ShapeDtypeStruct(ready_down.shape, ready_down.dtype),
+        in_specs=[pl.BlockSpec(memory_space=pltpu.VMEM), hbm],
+        out_specs=hbm,
+        scratch_shapes=[pltpu.SemaphoreType.DMA((late_down.shape[0],))],
+        input_output_aliases={1: 0},
         compiler_params=pltpu.CompilerParams(vmem_limit_bytes=8 * 2**20),
-        name="settle",
-    )(pltpu.with_memory_space_constraint(ready_down, pltpu.VMEM), scale, router)
+        name="place_late",
+    )(late_down, ready_down)
 
 
 def per_device(n, ne, train_down, other_down, router_weight, router_gain):
-    ready_down, scale, router = update(
+    ready_down, scale, router, late_down = update(
         train_down, other_down, router_weight.T, router_gain[None, :], n, ne
     )
+    late_down = lax.ppermute(late_down, "shard", [(s, (s + n // 2) % n) for s in range(n)])
     ready_down, scale_down, router = settle(ready_down, scale, router)
+    ready_down = place_late(late_down, ready_down, n)
     return (ready_down, scale_down, router.T)
 
 

time: 590 us -> 582 us (0.986)
  Pallas kernels: 589 us -> 573 us
  waiting for transfers between devices: 0 us -> 7.69 us
    pallas_call x1 -> x2, Pallas kernels: 579 us -> 564 us  [the longest x1 564 us: update(): pl.pallas_call(functools.partial(update_kernel, n, ne, r, head, group, la...]
    ppermute x0 -> x1, waiting for transfers between devices: none -> 7.69 us  [per_device(): lax.ppermute(late_down, 'shard', [(s, (s + n // 2) % n) for s in range(n)])]
  transfers between devices with their start and end apart: 0 -> 1, of which waited for: 0 -> 1; matrix products, arithmetic and copies ran while one was open for 0% -> 0% of each run, Pallas kernels for 0% -> 2%
where the time goes in v3:
time: 582 us; the launch traced here: 581 us
  Pallas kernels  573 us (98%)
  waiting for transfers between devices  7.69 us (1%)
    pallas_call x1, Pallas kernels, update(): pl.pallas_call(functools.partial(update_kernel, n, ne, r, head, group, la...  564 us
  transfers between devices with their start and end apart: 1, of which 1 were waited for; matrix products, arithmetic and copies ran while one was open for 0% of the time, Pallas kernels for 2%

profile of v3, /device:TPU:0, one launch (start us, length us, event | category | flops | bytes accessed | tf_op | source)
XLA Modules:
  0.0 581.5 jit_solution(9689918579582010701)
XLA Ops:
  0.6 563.6 %update.1 = (bf16[4,800,4096]{2,1,0:T(8,128)(2,1)S(1)}, f32[40,1,128]{2,1,0:T(1,128)S(1)}, bf16[4,4,4096]{2,1,0:T(4,128)(2,1)S(1)}, bf16[4,80,512]{2,1,0:T(8,128)(2,1)S(1)}) custom-call(f32[4,8,800,512]{3,2,1,0:T(8,128)} %bitcast.5, bf16[4,8,800,512]{3,2,1,0:T(8,128)(2,1)} %bitcast.6, f32[4,512]{1,0:T(4,128)} %bitcast.7, f32[1,512]{1,0:T(1,128)} %bitcast.8), custom_call_target="tpu_custom_call" | custom-call | tf_op jit(solution)/shard_map/update/pallas_call | solution.py:416
  564.2 0.1 collective-permute-start
  564.3 8.7 %settle.1 = (bf16[4,800,4096]{2,1,0:T(8,128)(2,1)}, f32[4,800]{1,0:T(4,128)}, bf16[16,4096]{1,0:T(8,128)(2,1)}) custom-call(bf16[4,800,4096]{2,1,0:T(8,128)(2,1)S(1)} %get-tuple-element.11.ready_ref, f32[40,1,128]{2,1,0:T(1,128)S(1)} %get-tuple-element.12.scale_ref, bf16[4,4,4096]{2,1,0:T(4,128)(2,1)S(1)} %get-tuple-element.13.router_ref), custom_call_target="tpu_custom_call" | custom-call | flops 100000000 | bytes 26214400 | tf_op jit(solution)/shard_map/settle/pallas_call | solution.py:506
  573.1 7.7 %collective-permute-done.late_ref = bf16[4,80,512]{2,1,0:T(8,128)(2,1)S(1)} collective-permute-done((bf16[4,80,512]{2,1,0:T(8,128)(2,1)S(1)}, bf16[4,80,512]{2,1,0:T(8,128)(2,1)S(1)}, u32[]{:S(2)}, u32[]{:S(2)}) %collective-permute-start) | collective-permute-done | bytes 327712 | tf_op jit(solution)/shard_map/ppermute | solution.py:557
  580.7 0.8 place_late.1
Async XLA Ops:
  564.2 16.5 %collective-permute-start = (bf16[4,80,512]{2,1,0:T(8,128)(2,1)S(1)}, bf16[4,80,512]{2,1,0:T(8,128)(2,1)S(1)}, u32[]{:S(2)}, u32[]{:S(2)}) collective-permute-start(bf16[4,80,512]{2,1,0:T(8,128)(2,1)S(1)} %get-tuple-element.10), channel_id=1, source_target_pairs={{0,4},{1,5},{2,6},{3,7},{4,0},{5,1},{6,2},{7,3},{8,12},{9,13},{10,... | collective-permute-start | bytes 983048 | tf_op jit(solution)/shard_map/ppermute | solution.py:557

commit v4 on v3

--- a/solution.py
+++ b/solution.py
@@ -9,7 +9,7 @@
 
 LANES = 128
 UNIT = 128
-RING = 4
+RING = 6
 HEAD = 4
 GROUP = 12
 LAGS = (7, 4, 2)
@@ -251,7 +251,8 @@
             m = jnp.where(is_late & (m > 0), swapped, m)
             far = m < half
             t = jnp.where(far, 1 - side, side)
-            q = lax.rem(place + jnp.where(far, m, m - half + 1), half)
+            turn = jnp.where(far & jnp.logical_not(is_late), lax.rem(my_e, 2) * (half // 2), 0)
+            q = lax.rem(place + turn + jnp.where(far, m, m - half + 1), half)
             return t, q
 
         def piece(t, q):

time: 582 us -> 582 us (level)
  no operation moved by 1% of the time
where the time goes in v4:
time: 582 us; the launch traced here: 581 us
  Pallas kernels  574 us (99%)
  waiting for transfers between devices  7.19 us (1%)
    pallas_call x1, Pallas kernels, update(): pl.pallas_call(functools.partial(update_kernel, n, ne, r, head, group, la...  564 us
  transfers between devices with their start and end apart: 1, of which 1 were waited for; matrix products, arithmetic and copies ran while one was open for 0% of the time, Pallas kernels for 2%

profile of v4, /device:TPU:0, one launch (start us, length us, event | category | flops | bytes accessed | tf_op | source)
XLA Modules:
  0.0 581.4 jit_solution(10750263659957288969)
XLA Ops:
  0.6 564.0 %update.1 = (bf16[4,800,4096]{2,1,0:T(8,128)(2,1)S(1)}, f32[40,1,128]{2,1,0:T(1,128)S(1)}, bf16[4,4,4096]{2,1,0:T(4,128)(2,1)S(1)}, bf16[4,80,512]{2,1,0:T(8,128)(2,1)S(1)}) custom-call(f32[4,8,800,512]{3,2,1,0:T(8,128)} %bitcast.5, bf16[4,8,800,512]{3,2,1,0:T(8,128)(2,1)} %bitcast.6, f32[4,512]{1,0:T(4,128)} %bitcast.7, f32[1,512]{1,0:T(1,128)} %bitcast.8), custom_call_target="tpu_custom_call" | custom-call | tf_op jit(solution)/shard_map/update/pallas_call | solution.py:417
  564.7 0.1 collective-permute-start
  564.8 8.7 %settle.1 = (bf16[4,800,4096]{2,1,0:T(8,128)(2,1)}, f32[4,800]{1,0:T(4,128)}, bf16[16,4096]{1,0:T(8,128)(2,1)}) custom-call(bf16[4,800,4096]{2,1,0:T(8,128)(2,1)S(1)} %get-tuple-element.11.ready_ref, f32[40,1,128]{2,1,0:T(1,128)S(1)} %get-tuple-element.12.scale_ref, bf16[4,4,4096]{2,1,0:T(4,128)(2,1)S(1)} %get-tuple-element.13.router_ref), custom_call_target="tpu_custom_call" | custom-call | flops 100000000 | bytes 26214400 | tf_op jit(solution)/shard_map/settle/pallas_call | solution.py:507
  573.5 7.2 %collective-permute-done.late_ref = bf16[4,80,512]{2,1,0:T(8,128)(2,1)S(1)} collective-permute-done((bf16[4,80,512]{2,1,0:T(8,128)(2,1)S(1)}, bf16[4,80,512]{2,1,0:T(8,128)(2,1)S(1)}, u32[]{:S(2)}, u32[]{:S(2)}) %collective-permute-start) | collective-permute-done | bytes 327712 | tf_op jit(solution)/shard_map/ppermute | solution.py:558
  580.7 0.8 place_late.1
Async XLA Ops:
  564.7 16.0 %collective-permute-start = (bf16[4,80,512]{2,1,0:T(8,128)(2,1)S(1)}, bf16[4,80,512]{2,1,0:T(8,128)(2,1)S(1)}, u32[]{:S(2)}, u32[]{:S(2)}) collective-permute-start(bf16[4,80,512]{2,1,0:T(8,128)(2,1)S(1)} %get-tuple-element.10), channel_id=1, source_target_pairs={{0,4},{1,5},{2,6},{3,7},{4,0},{5,1},{6,2},{7,3},{8,12},{9,13},{10,... | collective-permute-start | bytes 983048 | tf_op jit(solution)/shard_map/ppermute | solution.py:558
